TPU v7x, 32 devices: a whole 2x2x4 slice. The times are simulated.
32 devices in a mesh: fit: 4 (over z), pair: 8 (over y, x, core).
Axes of the slice: x: 2, y: 2, z: 4, core: 2. Of those that a mesh axis runs over, the one named last changes fastest.
Arguments:
- metric_factor: bfloat16 [4096, 4096], P('fit'), as said below
- three_index: bfloat16 [4096, 16384], P('fit', 'pair'), may hold values from -6 to 6
- send_map: int32 [8, 8, 16], P('pair'), may hold values from 0 to 15
- pair_slots: int32 [8, 128], P('pair'), may hold values from 0 to 127, each once within a row
- pair_count: int32 [8], P('pair'), may hold values from 1 to 64, 256 in all
- orbital_energy: bfloat16 [128], P('pair'), may hold values from -2 to -0.19921875
- cabs_energy: float32 [1024], replicated, may hold values from 0.5 to 4
- coupling: bfloat16 [128, 1024], replicated, may hold values from -0.5 to 0.5
Outputs:
- projected: bfloat16 [8, 64, 128, 1024], P('pair', 'fit')
Inputs may be any that keep to these rules, and one draw needn't show every extreme that they name: `metric_factor`: diagonal entries lie between 0.6 and 1.4. `pair_slots`: each row holds every position 0 to 127 once; pair n of a row uses entries 2n and 2n + 1.
All inputs are finite; a program needn't handle non-finite values. No bound on the sum of `pair_count` on one device may be relied on, other than what follows from the above.
Results may differ from a plain program's by a relative error of at most 0.015.
Values may be sent and summed in bfloat16 or wider, within the bound.
No kernel may reach another device: no remote copies, remote signals or barrier semaphores. Data moves between devices by JAX's collectives and lax.ppermute only.
A program may use at most 256 MiB of HBM per device.

v0:
```python
import jax
import jax.numpy as jnp
from jax import lax
from jax.sharding import PartitionSpec as P

NAUX = 4096
PAIR_BLOCK = 8


def on_device(
    metric_factor,
    three_index,
    send_map,
    pair_slots,
    pair_count,
    orbital_energy,
    cabs_energy,
    coupling,
):
    domain = coupling.shape[0]
    orbitals = orbital_energy.shape[0]
    local_rows = metric_factor.shape[0]
    peers = send_map.shape[1]
    capacity = send_map.shape[2]
    slot_total = pair_slots.shape[1] // 2
    fitted = jnp.dot(
        metric_factor,
        lax.all_gather(three_index, "fit", axis=0, tiled=True),
        preferred_element_type=jnp.float32,
    )
    fitted = fitted.astype(jnp.bfloat16).reshape(local_rows, orbitals, domain)
    requests = send_map.reshape(peers, capacity)
    source, energy_src = (
        lax.all_gather(fitted, "pair", axis=1, tiled=True),
        lax.all_gather(orbital_energy, "pair", axis=0, tiled=True),
    )
    global_ids = (jnp.arange(peers, dtype=jnp.int32)[:, None] * orbitals + requests).reshape(-1)
    pair_index = jnp.take(global_ids, pair_slots[0])
    left_index = pair_index[0::2]
    right_index = pair_index[1::2]
    live_count = pair_count[0]
    norm_scale = NAUX ** (-0.5)
    block_count = (live_count + PAIR_BLOCK - 1) // PAIR_BLOCK

    def advance(block, partial_value):
        left_ids = lax.dynamic_slice_in_dim(left_index, block * PAIR_BLOCK, PAIR_BLOCK)
        right_ids = lax.dynamic_slice_in_dim(right_index, block * PAIR_BLOCK, PAIR_BLOCK)
        left_rows = jnp.take(source, left_ids, axis=1)
        right_rows = jnp.take(source, right_ids, axis=1)
        product = jnp.einsum(
            "qsa,qsb->sab", left_rows, right_rows, preferred_element_type=jnp.float32
        )
        return lax.dynamic_update_slice_in_dim(
            partial_value, product * norm_scale, block * PAIR_BLOCK, 0
        )

    partial_value = jnp.zeros((slot_total, domain, domain), jnp.float32)
    partial_value = lax.fori_loop(0, block_count, advance, partial_value)
    share = slot_total // lax.axis_size("fit")
    first_slot = lax.axis_index("fit") * share
    totals = lax.psum(partial_value.astype(jnp.bfloat16), "fit").astype(jnp.float32)
    exchange = lax.dynamic_slice_in_dim(totals, first_slot, share, 0)
    energy_sum = jnp.take(energy_src, left_index).astype(jnp.float32) + jnp.take(
        energy_src, right_index
    ).astype(jnp.float32)
    energy_sum = lax.dynamic_slice_in_dim(energy_sum, first_slot, share, 0)
    weighted = jnp.einsum(
        "sab,bc->sac", exchange.astype(jnp.bfloat16), coupling, preferred_element_type=jnp.float32
    )
    denom = cabs_energy[None, None, :] - energy_sum[:, None, None]
    live_mask = first_slot + jnp.arange(share, dtype=jnp.int32) < live_count
    projected = jnp.where(live_mask[:, None, None], weighted / denom, 0.0).astype(jnp.bfloat16)
    return projected.reshape(1, share, domain, weighted.shape[2])


def solution(mesh):
    in_specs = (
        P("fit", None),
        P("fit", "pair"),
        P("pair", None, None),
        P("pair", None),
        P("pair"),
        P("pair"),
        P(),
        P(),
    )
    out_specs = P("pair", "fit", None, None)
    return jax.shard_map(
        on_device, mesh=mesh, in_specs=in_specs, out_specs=out_specs, check_vma=False
    )
```

profile of v0, /device:TPU:0, one launch (start us, length us, event | category | flops | bytes accessed | tf_op | source)
XLA Modules:
  0.0 655.6 jit_solution(15301180865822851365)
XLA Ops:
  6.5 0.0 copy-start
  6.5 0.0 all-gather.3.cloned.1.call-start
  6.5 0.7 all-gather.3.cloned.1.call-update
  7.3 0.0 all-gather.5.cloned.1.call-start
  7.3 291.1 %all-gather.3.cloned.1.call-done = bf16[4096,2048]{1,0:T(8,128)(2,1)} async-done(((bf16[1024,2048]{1,0:T(8,128)(2,1)}), bf16[4096,2048]{1,0:T(8,128)(2,1)}) %all-gather.3.cloned.1.call-update) | async-done | bytes 16777232 | tf_op jit(solution)/shard_map/all_gather | solution.py:28
  298.4 22.7 %convert_bitcast_fusion = bf16[128,16,8,128]{3,2,1,0:T(8,128)(2,1)S(1)} fusion(bf16[1024,4096]{1,0:T(8,128)(2,1)} %param.14, bf16[4096,2048]{1,0:T(8,128)(2,1)} %all-gather.3.cloned.1.call-done), kind=kOutput, calls=%fused_computation.24 | convolution fusion | flops 17181966336 | bytes 29360128 | tf_op jit(solution)/shard_map/dot_general | solution.py:26
  321.1 3.1 copy.18
  324.2 0.0 copy-start.2
  324.2 0.0 copy-start.3
  324.2 0.0 all-gather.5.cloned.1.call-update
  324.2 0.0 all-reduce.3.cloned.1.call-start
  325.0 0.1 add.77
  325.0 0.1 add.78
  325.1 0.0 copy-done.2
  325.1 0.1 reshape.94
  325.2 0.0 copy-done.3
  325.2 1.2 gather_fusion.2
  326.5 0.2 slice.6
  326.6 0.2 slice.7
  326.8 156.4 %all-gather.5.cloned.1.call-done = bf16[1024,128,128]{2,0,1:T(8,128)(2,1)} async-done(((bf16[1024,16,128]{2,0,1:T(8,128)(2,1)}), bf16[1024,128,128]{2,0,1:T(8,128)(2,1)}) %all-gather.5.cloned.1.call-update) | async-done | bytes 33554448 | tf_op jit(solution)/shard_map/all_gather | solution.py:34
  483.2 1.8 broadcast_in_dim.41
  485.1 9.2 %while.10 = (s32[]{:T(128)}, bf16[64,128,128]{2,1,0:T(8,128)(2,1)}, s32[]{:T(128)}, s32[64]{0:T(128)S(1)}, bf16[1024,128,128]{2,0,1:T(8,128)(2,1)}, /*index=5*/s...) while((s32[]{:T(128)}, bf16[64,128,128]{2,1,0:T(8,128)(2,1)}, s32[]{:T(128)}, s32[64]{0:T(128)S(1)}, ...), condition=%wide.region_1.3_spmd, body=%wide.region_0.0_spmd.sunk | while | flops 270665824 | bytes 13115835 | solution.py:58
  485.1 0.1 compare_and_fusion.3
  485.2 2.4 gather_fusion
  487.5 3.5 gather_fusion.1
  491.1 3.2 fusion.31
  494.3 0.0 copy-start.5
  494.3 0.0 copy-start.4
  494.3 0.0 copy-start.1
  494.3 0.0 all-reduce.3.cloned.1.call-update
  494.3 0.6 copy-done.5
  495.0 0.6 dynamic-slice
  496.3 0.0 copy-done.4
  496.3 0.2 dynamic-update-slice
  496.6 77.8 %all-reduce = bf16[128]{0:T(256)(128)(2,1)S(1)} all-reduce(bf16[128]{0:T(256)(128)(2,1)S(1)} %dynamic-update-slice), channel_id=1, replica_groups=mesh['fit'=4,'pair'=8] {'pair'}, use_global_device_ids=true, to_apply=%add | all-reduce | flops 128 | bytes 512
  574.3 0.8 gather_fusion.3
  575.1 0.8 gather_fusion.4
  575.9 0.1 dynamic_slice.13
  576.0 0.0 copy-done.1
  576.0 0.1 broadcast_subtract_fusion
  576.1 68.7 %all-reduce.3.cloned.1.call-done = bf16[64,128,128]{2,1,0:T(8,128)(2,1)} async-done(((bf16[64,128,128]{2,1,0:T(8,128)(2,1)}), bf16[64,128,128]{2,1,0:T(8,128)(2,1)}) %all-reduce.3.cloned.1.call-update) | async-done | bytes 2097168 | tf_op jit(solution)/shard_map/psum | solution.py:61
  644.8 0.0 copy-done
  644.8 4.3 fusion.19
  (14 shorter events, 0.1 us)
Async XLA Ops:
  6.5 638.2 %copy-start = (bf16[128,1024]{1,0:T(8,128)(2,1)S(1)}, bf16[128,1024]{1,0:T(8,128)(2,1)}, u32[]{:S(2)}) copy-start(bf16[128,1024]{1,0:T(8,128)(2,1)} %param.21) | copy-start | bytes 786436
  6.5 291.9 %all-gather.3.cloned.1.call-start = ((), (), s32[]{:S(2)}) async-start(), calls=%async_computation | async-start | bytes 20971520 | tf_op jit(solution)/shard_map/all_gather | solution.py:28
  7.3 476.0 %all-gather.5.cloned.1.call-start = ((), (), s32[]{:S(2)}) async-start(), calls=%async_computation.1 | async-start | bytes 37748736 | tf_op jit(solution)/shard_map/all_gather | solution.py:34
  324.2 0.9 copy-start.2
  324.2 1.0 copy-start.3
  324.2 320.5 %all-reduce.3.cloned.1.call-start = ((), (), s32[]{:S(2)}) async-start(), calls=%async_computation.2 | async-start | bytes 4194304 | tf_op jit(solution)/shard_map/psum | solution.py:61
  494.3 0.7 copy-start.5
  494.3 2.0 copy-start.4
  494.3 81.7 %copy-start.1 = (f32[1024]{0:T(1024)S(1)}, f32[1024]{0:T(1024)}, u32[]{:S(2)}) copy-start(f32[1024]{0:T(1024)} %param.20) | copy-start | bytes 12292
Sparse Core Ops, SparseCore 0:
  8.9 289.4 all-gather.2
  324.4 158.8 all-gather.4
  494.5 150.2 all-reduce.2
where the time goes:
time: 657 us; the launch traced here: 656 us
  waiting for transfers between devices  517 us (79%)
  blocking collectives  77.8 us (12%)
  matrix products  30.2 us (5%)
  local copies, waits for them, and re-layouts  15.8 us (2%)
  between operations  14.6 us (2%)
    all_gather x1, waiting for transfers between devices, on_device(): lax.all_gather(three_index, 'fit', axis=0, tiled=True)  291 us
    all_gather x1, waiting for transfers between devices, on_device(): lax.all_gather(fitted, 'pair', axis=1, tiled=True)  156 us
    unnamed x1, blocking collectives  77.8 us
    psum x1, waiting for transfers between devices, on_device(): lax.psum(partial_value.astype(jnp.bfloat16), 'fit').astype(jnp.float32)  68.7 us
    dot_general x1, matrix products, on_device(): jnp.dot(metric_factor, lax.all_gather(three_index, 'fit', axis=0, tiled=T...  22.7 us
  transfers between devices with their start and end apart: 3, of which 3 were waited for; matrix products, arithmetic and copies ran while one was open for 1% of the time, Pallas kernels for 0%

commit v1 on v0

--- a/solution.py
+++ b/solution.py
@@ -58,7 +58,9 @@
     partial_value = lax.fori_loop(0, block_count, advance, partial_value)
     share = slot_total // lax.axis_size("fit")
     first_slot = lax.axis_index("fit") * share
-    totals = lax.psum(partial_value.astype(jnp.bfloat16), "fit").astype(jnp.float32)
+    totals = jnp.sum(lax.all_gather(partial_value.astype(jnp.bfloat16), "fit"), axis=0).astype(
+        jnp.float32
+    )
     exchange = lax.dynamic_slice_in_dim(totals, first_slot, share, 0)
     energy_sum = jnp.take(energy_src, left_index).astype(jnp.float32) + jnp.take(
         energy_src, right_index

time: 657 us -> 725 us (1.10)
  waiting for transfers between devices: 517 us -> 581 us
    all_gather x0 -> x1, waiting for transfers between devices: none -> 133 us  [on_device(): lax.all_gather(partial_value.astype(jnp.bfloat16), 'fit')]
    psum x1 -> x0, waiting for transfers between devices: 68.7 us -> none  [on_device(): lax.psum(partial_value.astype(jnp.bfloat16), 'fit').astype(jnp.float32)]
where the time goes in v1:
time: 725 us; the launch traced here: 724 us
  waiting for transfers between devices  581 us (80%)
  blocking collectives  77.4 us (11%)
  matrix products  29.2 us (4%)
  local copies, waits for them, and re-layouts  15.7 us (2%)
  between operations  14.5 us (2%)
    all_gather x1, waiting for transfers between devices, on_device(): lax.all_gather(three_index, 'fit', axis=0, tiled=True)  291 us
    all_gather x1, waiting for transfers between devices, on_device(): lax.all_gather(fitted, 'pair', axis=1, tiled=True)  156 us
    all_gather x1, waiting for transfers between devices, on_device(): lax.all_gather(partial_value.astype(jnp.bfloat16), 'fit')  133 us
    unnamed x1, blocking collectives  77.4 us
    dot_general x1, matrix products, on_device(): jnp.dot(metric_factor, lax.all_gather(three_index, 'fit', axis=0, tiled=T...  22.7 us
  transfers between devices with their start and end apart: 3, of which 3 were waited for; matrix products, arithmetic and copies ran while one was open for 1% of the time, Pallas kernels for 0%

profile of v1, /device:TPU:0, one launch (start us, length us, event | category | flops | bytes accessed | tf_op | source)
XLA Modules:
  0.0 723.7 jit_solution(7343074045544064265)
XLA Ops:
  6.5 0.0 copy-start
  6.5 0.0 all-gather.5.cloned.1.call-start
  6.5 0.7 all-gather.5.cloned.1.call-update
  7.3 0.0 all-gather.7.cloned.1.call-start
  7.3 291.1 %all-gather.5.cloned.1.call-done = bf16[4096,2048]{1,0:T(8,128)(2,1)} async-done(((bf16[1024,2048]{1,0:T(8,128)(2,1)}), bf16[4096,2048]{1,0:T(8,128)(2,1)}) %all-gather.5.cloned.1.call-update) | async-done | bytes 16777232 | tf_op jit(solution)/shard_map/all_gather | solution.py:28
  298.4 22.7 %convert_bitcast_fusion = bf16[128,16,8,128]{3,2,1,0:T(8,128)(2,1)S(1)} fusion(bf16[1024,4096]{1,0:T(8,128)(2,1)} %param.14, bf16[4096,2048]{1,0:T(8,128)(2,1)} %all-gather.5.cloned.1.call-done), kind=kOutput, calls=%fused_computation.24 | convolution fusion | flops 17181966336 | bytes 29360128 | tf_op jit(solution)/shard_map/dot_general | solution.py:26
  321.1 3.1 copy.18
  324.2 0.0 copy-start.2
  324.2 0.0 copy-start.3
  324.2 0.0 all-gather.7.cloned.1.call-update
  324.2 0.0 all-gather.9.cloned.1.call-start
  324.9 0.1 add.75
  325.0 0.1 add.76
  325.1 0.0 copy-done.2
  325.1 0.1 reshape.94
  325.2 0.0 copy-done.3
  325.2 1.2 gather_fusion.2
  326.5 0.2 slice.6
  326.6 0.2 slice.7
  326.8 156.4 %all-gather.7.cloned.1.call-done = bf16[1024,128,128]{2,0,1:T(8,128)(2,1)} async-done(((bf16[1024,16,128]{2,0,1:T(8,128)(2,1)}), bf16[1024,128,128]{2,0,1:T(8,128)(2,1)}) %all-gather.7.cloned.1.call-update) | async-done | bytes 33554448 | tf_op jit(solution)/shard_map/all_gather | solution.py:34
  483.2 1.8 broadcast_in_dim.41
  485.1 9.2 %while.10 = (s32[]{:T(128)}, bf16[64,128,128]{2,1,0:T(8,128)(2,1)}, s32[]{:T(128)}, s32[64]{0:T(128)S(1)}, bf16[1024,128,128]{2,0,1:T(8,128)(2,1)}, /*index=5*/s...) while((s32[]{:T(128)}, bf16[64,128,128]{2,1,0:T(8,128)(2,1)}, s32[]{:T(128)}, s32[64]{0:T(128)S(1)}, ...), condition=%wide.region_1.3_spmd, body=%wide.region_0.0_spmd.sunk | while | flops 270665824 | bytes 13115835 | solution.py:58
  485.1 0.1 compare_and_fusion.3
  485.2 2.4 gather_fusion
  487.5 3.5 gather_fusion.1
  491.1 3.2 fusion.31
  494.3 0.0 copy-start.5
  494.3 0.0 copy-start.4
  494.3 0.0 copy-start.1
  494.3 0.0 all-gather.9.cloned.1.call-update
  494.3 0.6 copy-done.5
  495.0 0.6 dynamic-slice
  496.1 0.0 copy-done.4
  496.1 0.2 dynamic-update-slice
  496.4 77.4 %all-reduce = bf16[128]{0:T(256)(128)(2,1)S(1)} all-reduce(bf16[128]{0:T(256)(128)(2,1)S(1)} %dynamic-update-slice), channel_id=1, replica_groups=mesh['fit'=4,'pair'=8] {'pair'}, use_global_device_ids=true, to_apply=%add | all-reduce | flops 128 | bytes 512
  573.8 0.8 gather_fusion.3
  574.5 0.8 gather_fusion.4
  575.3 0.1 dynamic_slice.13
  575.4 0.0 copy-done.1
  575.4 0.1 broadcast_subtract_fusion
  575.5 132.7 %all-gather.9.cloned.1.call-done = bf16[256,128,128]{2,1,0:T(8,128)(2,1)} async-done(((bf16[64,128,128]{2,1,0:T(8,128)(2,1)}), bf16[256,128,128]{2,1,0:T(8,128)(2,1)}) %all-gather.9.cloned.1.call-update) | async-done | bytes 8388624 | tf_op jit(solution)/shard_map/all_gather | solution.py:61
  708.2 5.7 reduce_sum.12
  713.9 0.0 copy-done
  713.9 3.3 fusion.19
  (14 shorter events, 0.1 us)
Async XLA Ops:
  6.5 707.4 %copy-start = (bf16[128,1024]{1,0:T(8,128)(2,1)S(1)}, bf16[128,1024]{1,0:T(8,128)(2,1)}, u32[]{:S(2)}) copy-start(bf16[128,1024]{1,0:T(8,128)(2,1)} %param.21) | copy-start | bytes 786436
  6.5 291.9 %all-gather.5.cloned.1.call-start = ((), (), s32[]{:S(2)}) async-start(), calls=%async_computation | async-start | bytes 20971520 | tf_op jit(solution)/shard_map/all_gather | solution.py:28
  7.3 476.0 %all-gather.7.cloned.1.call-start = ((), (), s32[]{:S(2)}) async-start(), calls=%async_computation.1 | async-start | bytes 37748736 | tf_op jit(solution)/shard_map/all_gather | solution.py:34
  324.2 0.9 copy-start.2
  324.2 1.0 copy-start.3
  324.2 384.0 %all-gather.9.cloned.1.call-start = ((), (), s32[]{:S(2)}) async-start(), calls=%async_computation.2 | async-start | bytes 10485760 | tf_op jit(solution)/shard_map/all_gather | solution.py:61
  494.3 0.7 copy-start.5
  494.3 1.8 copy-start.4
  494.3 81.1 %copy-start.1 = (f32[1024]{0:T(1024)S(1)}, f32[1024]{0:T(1024)}, u32[]{:S(2)}) copy-start(f32[1024]{0:T(1024)} %param.20) | copy-start | bytes 12292
Sparse Core Ops, SparseCore 0:
  8.9 289.4 all-gather.4
  324.4 158.8 all-gather.6
  494.5 213.7 all-gather.8
